TPU v7x, 256 devices: a whole 4x4x8 slice. The times are simulated.
256 devices in a mesh: blk: 128 (over y, z, x_hi, core), mp: 2 (over x_lo).
Axes of the slice: x: 4 (x_hi: 2, x_lo: 2; x = x_hi * 2 + x_lo), y: 4, z: 8, core: 2. Of those that a mesh axis runs over, the one named last changes fastest.
Arguments:
- params: bfloat16 [128, 1024, 4096], P('blk', None, 'mp'), may hold values from -0.09375 to 0.09375
- hidden: bfloat16 [128, 384, 4096], P('blk', None, 'mp'), may hold values from -6 to 6
- targets: bfloat16 [128, 384, 1024], P('blk', None, 'mp'), may hold values from -6 to 6
Outputs:
- params_out: bfloat16 [128, 1024, 4096], P('blk', None, 'mp')
- errors: float32 [2], replicated
All inputs are finite; a program needn't handle non-finite values.
Results may differ from a plain program's by a relative error of at most 0.0085.
Values may be sent and summed in bfloat16 or wider, within the bound.
A program may use at most 128 MiB of HBM per device.

v0:
```python
import functools

import jax
import jax.numpy as jnp
from jax import lax
from jax.sharding import Mesh
from jax.sharding import PartitionSpec as P

ITERS = 2
BLK = ("blk_0", "blk_1", "blk_2", "blk_3")
BLK_MP = ("blk_0", "blk_1", "blk_2", "blk_3", "mp")


mix_third = 1.0 / 3.0
step_size = 0.1


def from_behind(block, axis, distance):
    devices = range(lax.axis_size(axis))
    route = [((i - distance) % len(devices), i) for i in devices]
    return lax.ppermute(block, axis, route)


def from_everyone(x, axis):
    copies = jnp.broadcast_to(x, (lax.axis_size(axis), *x.shape))
    return lax.all_to_all(copies, axis, split_axis=0, concat_axis=0, tiled=True)


def taken_together(x, axis):
    return from_everyone(x, axis).sum(axis=0)


def over_axes(x, axes):
    return functools.reduce(lax.psum, axes, x)


def send_tracker(track):
    track_left = from_behind(track, BLK, 1)
    track_right = from_behind(track, BLK, -1)
    return (track_left, track_right)


def on_device(params, hidden, targets):
    state = params[0]
    feats = hidden[0]
    targ_local = targets[0]
    tokens = feats.shape[0]
    hidden_total = state.shape[1] * lax.axis_size("mp")
    replicas = lax.axis_size(BLK)
    full_targ = lax.all_gather(targ_local, "mp", axis=1, tiled=True)

    def gradient(weight):
        partial_value = lax.dot_general(
            feats, weight, (((1,), (1,)), ((), ())), preferred_element_type=jnp.float32
        )
        output = taken_together(partial_value, "mp")
        resid = (output - full_targ.astype(jnp.float32)).astype(jnp.bfloat16)
        grad = lax.dot_general(
            resid, feats, (((0,), (0,)), ((), ())), preferred_element_type=jnp.float32
        )
        return grad / tokens

    older = gradient(state)
    fresh = older
    track = older.astype(jnp.bfloat16)
    track_left, track_right = send_tracker(track)
    err_list = []
    for step in range(ITERS):
        state_left = from_behind(state, BLK, 1)
        state_right = from_behind(state, BLK, -1)
        if step > 0:
            track_mix = (
                track_left.astype(jnp.float32)
                + track.astype(jnp.float32)
                + track_right.astype(jnp.float32)
            ) * mix_third
            track = (track_mix + fresh - older).astype(jnp.bfloat16)
            older = fresh
        own_state = state.astype(jnp.float32)
        diff = own_state - state_right.astype(jnp.float32)
        local_err = jnp.sum(diff * diff) / (hidden_total * replicas)
        err_list.append(local_err)
        blended = (
            state_left.astype(jnp.float32) + own_state + state_right.astype(jnp.float32)
        ) * mix_third
        new_state = (blended - step_size * track.astype(jnp.float32)).astype(jnp.bfloat16)
        if step < ITERS - 1:
            fresh = gradient(new_state)
        state = new_state
    errors = jnp.stack(err_list)
    errors = over_axes(errors, BLK_MP)
    return (state[None], errors)


def solution(mesh):
    torus = Mesh(
        mesh.devices.reshape(4, 8, 2, 2, mesh.shape["mp"]),
        ("blk_0", "blk_1", "blk_2", "blk_3", "mp"),
    )
    placed = (P(BLK, None, "mp"), P(BLK, None, "mp"), P(BLK, None, "mp"))
    return jax.shard_map(
        on_device, mesh=torus, in_specs=placed, out_specs=(P(BLK, None, "mp"), P()), check_vma=False
    )
```

profile of v0, /device:TPU:194, one launch (start us, length us, event | category | flops | bytes accessed | tf_op | source)
XLA Modules:
  0.0 420.3 jit_solution(9891182136154639013)
XLA Ops:
  0.6 0.0 copy-start
  0.6 2.1 collective-permute-start.1
  2.7 0.0 collective-permute-start
  2.7 4.0 fusion.23
  6.8 2.1 broadcast_in_dim.9
  8.8 6.8 %all-to-all-start = ((f32[2,384,1024]{2,1,0:T(8,128)}), f32[2,384,1024]{2,1,0:T(8,128)}, u32[]{:S(2)}, u32[]{:S(2)}) async-start(f32[2,384,1024]{2,1,0:T(8,128)} %broadcast_in_dim.9), calls=%async_computation | async-start | bytes 6291456 | tf_op jit(solution)/shard_map/all_to_all | solution.py:26
  15.6 78.1 %all-gather = bf16[1,384,1024]{2,1,0:T(8,128)(2,1)} all-gather(bf16[1,384,512]{2,1,0:T(8,128)(2,1)S(1)} %copy-done.2), channel_id=2, replica_groups=mesh['blk_0'=4,'blk_1'=8,'blk_2'=2,'blk_3'=2,'mp'=2] {'mp'}, dimensions={2}, use_global_device_ids=true | all-gather | bytes 1179648 | tf_op jit(solution)/shard_map/all_gather | solution.py:50
  93.6 0.0 all-to-all-done
  93.6 2.3 reduce_sum.36
  96.0 0.0 collective-permute-done.1
  96.0 0.0 collective-permute-done
  96.0 13.7 %fusion.4 = (f32[]{:T(128)}, bf16[1024,2048]{1,0:T(8,128)(2,1)}, bf16[1024,2048]{1,0:T(8,128)(2,1)}, f32[1024,2048]{1,0:T(8,128)}) fusion(bf16[1024,2048]{1,0:T(8,128)(2,1)} %collective-permute-done.1, bf16[1,1024,2048]{2,1,0:T(8,128)(2,1)} %param.3, bf16[1024,2048]{1,0:T(8,128)(2,1)} %collective-permute-done, bf16[1,384,2048]{2,1,0:T(8,128)(2,1)S(1)} %copy-done, ...), kind=kOutput, calls=%fused_computation.12 | convolution fusion | flops 1643249664 | bytes 33292292 | tf_op jit(solution)/shard_map/dot_general | solution.py:58
  109.7 3.0 collective-permute-start.3
  112.7 86.1 %collective-permute-start.4 = (bf16[1024,2048]{1,0:T(8,128)(2,1)}, bf16[1024,2048]{1,0:T(8,128)(2,1)}, u32[]{:S(2)}, u32[]{:S(2)}) collective-permute-start(bf16[1024,2048]{1,0:T(8,128)(2,1)} %get-tuple-element.4), channel_id=1, source_target_pairs={{254,0},{0,2},{2,4},{4,6},{6,8},{8,10},{10,12},{12,14},{14,16},{16... | collective-permute-start | bytes 12582920 | tf_op jit(solution)/shard_map/ppermute | solution.py:21
  198.8 0.0 collective-permute-start.5
  198.8 3.2 collective-permute-start.2
  202.1 4.0 fusion.25
  206.1 2.1 broadcast_in_dim.10
  208.2 6.6 %all-to-all-start.1 = ((f32[2,384,1024]{2,1,0:T(8,128)}), f32[2,384,1024]{2,1,0:T(8,128)}, u32[]{:S(2)}, u32[]{:S(2)}) async-start(f32[2,384,1024]{2,1,0:T(8,128)} %broadcast_in_dim.10), calls=%async_computation.1 | async-start | bytes 6291456 | tf_op jit(solution)/shard_map/all_to_all | solution.py:26
  215.4 0.0 collective-permute-done.3
  215.4 6.3 %fusion.14 = f32[]{:T(128)} fusion(bf16[1024,2048]{1,0:T(8,128)(2,1)} %collective-permute-done.3, bf16[1024,2048]{1,0:T(8,128)(2,1)} %get-tuple-element.3), kind=kLoop, calls=%fused_computation.22 | loop fusion | flops 10485759 | bytes 8388612 | tf_op jit(solution)/shard_map/reduce_sum | solution.py:81
  222.4 0.1 pad_maximum_fusion
  222.5 10.7 %psum.35 = f32[2]{0:T(128)S(1)} all-reduce(f32[2]{0:T(128)S(1)} %pad_maximum_fusion), channel_id=1, replica_groups=mesh['blk_0'=4,'blk_1'=8,'blk_2'=2,'blk_3'=2,'mp'=2] {'blk_0'}, use_global_device_ids=true, to_apply=%region_4.0 | all-reduce | flops 2 | bytes 16 | tf_op jit(solution)/shard_map/psum | solution.py:34
  233.2 22.5 %psum.36 = f32[2]{0:T(128)S(1)} all-reduce(f32[2]{0:T(128)S(1)} %psum.35), channel_id=1, replica_groups=mesh['blk_0'=4,'blk_1'=8,'blk_2'=2,'blk_3'=2,'mp'=2] {'blk_1'}, use_global_device_ids=true, to_apply=%region_5.0 | all-reduce | flops 2 | bytes 16 | tf_op jit(solution)/shard_map/psum | solution.py:34
  255.7 138.1 %psum.37 = f32[2]{0:T(128)S(1)} all-reduce(f32[2]{0:T(128)S(1)} %psum.36), channel_id=1, replica_groups=mesh['blk_0'=4,'blk_1'=8,'blk_2'=2,'blk_3'=2,'mp'=2] {'blk_2'}, use_global_device_ids=true, to_apply=%region_6.0 | all-reduce | flops 2 | bytes 16 | tf_op jit(solution)/shard_map/psum | solution.py:34
  393.7 2.4 psum.38
  396.2 0.0 all-to-all-done.1
  396.2 3.5 reduce_sum.37
  399.6 5.4 %psum.39 = f32[2]{0:T(128)} all-reduce(f32[2]{0:T(128)S(1)} %psum.38), channel_id=1, replica_groups=mesh['blk_0'=4,'blk_1'=8,'blk_2'=2,'blk_3'=2,'mp'=2] {'mp'}, use_global_device_ids=true, to_apply=%region_8.0 | all-reduce | flops 2 | bytes 16 | tf_op jit(solution)/shard_map/psum | solution.py:34
  405.1 0.0 collective-permute-done.4
  405.1 0.0 collective-permute-done.5
  405.1 15.3 %fusion.15 = bf16[1,1024,2048]{2,1,0:T(8,128)(2,1)} fusion(bf16[1024,2048]{1,0:T(8,128)(2,1)} %collective-permute-done.3, bf16[1024,2048]{1,0:T(8,128)(2,1)} %get-tuple-element.3, bf16[1024,2048]{1,0:T(8,128)(2,1)} %collective-permute-done.2, f32[1024,2048]{1,0:T(8,128)} %get-tuple-element.5, bf16[1024,2048]{1,0:T(8,128)(2,1)} %collective-permute-done.5, ...), kind=kOutput, calls=%fused_computation.24 | convolution fusion | flops 1657929728 | bytes 37486592 | tf_op jit(solution)/shard_map/dot_general | solution.py:58
  (6 shorter events, 0.0 us)
Async XLA Ops:
  0.6 2.1 copy-start
  0.6 95.3 %collective-permute-start.1 = (bf16[1024,2048]{1,0:T(8,128)(2,1)}, bf16[1024,2048]{1,0:T(8,128)(2,1)}, u32[]{:S(2)}, u32[]{:S(2)}) collective-permute-start(bf16[1024,2048]{1,0:T(8,128)(2,1)} %bitcast.37), channel_id=1, source_target_pairs={{2,0},{4,2},{6,4},{8,6},{10,8},{12,10},{14,12},{16,14},{18,16},{20... | collective-permute-start | bytes 12582920 | tf_op jit(solution)/shard_map/ppermute | solution.py:21
  2.7 93.2 %collective-permute-start = (bf16[1024,2048]{1,0:T(8,128)(2,1)}, bf16[1024,2048]{1,0:T(8,128)(2,1)}, u32[]{:S(2)}, u32[]{:S(2)}) collective-permute-start(bf16[1024,2048]{1,0:T(8,128)(2,1)} %bitcast.38), channel_id=1, source_target_pairs={{254,0},{0,2},{2,4},{4,6},{6,8},{8,10},{10,12},{12,14},{14,16},{16... | collective-permute-start | bytes 12582920 | tf_op jit(solution)/shard_map/ppermute | solution.py:21
  8.8 6.8 %copy-start.2 = (bf16[1,384,512]{2,1,0:T(8,128)(2,1)S(1)}, bf16[1,384,512]{2,1,0:T(8,128)(2,1)}, u32[]{:S(2)}) copy-start(bf16[1,384,512]{2,1,0:T(8,128)(2,1)} %param.5) | copy-start | bytes 1179652
  8.8 84.8 %all-to-all-start = ((f32[2,384,1024]{2,1,0:T(8,128)}), f32[2,384,1024]{2,1,0:T(8,128)}, u32[]{:S(2)}, u32[]{:S(2)}) async-start(f32[2,384,1024]{2,1,0:T(8,128)} %broadcast_in_dim.9), calls=%async_computation | async-start | bytes 6291456 | tf_op jit(solution)/shard_map/all_to_all | solution.py:26
  109.7 105.7 %collective-permute-start.3 = (bf16[1024,2048]{1,0:T(8,128)(2,1)}, bf16[1024,2048]{1,0:T(8,128)(2,1)}, u32[]{:S(2)}, u32[]{:S(2)}) collective-permute-start(bf16[1024,2048]{1,0:T(8,128)(2,1)} %get-tuple-element.3), channel_id=1, source_target_pairs={{2,0},{4,2},{6,4},{8,6},{10,8},{12,10},{14,12},{16,14},{18,16},{20... | collective-permute-start | bytes 12582920 | tf_op jit(solution)/shard_map/ppermute | solution.py:21
  112.7 292.4 %collective-permute-start.4 = (bf16[1024,2048]{1,0:T(8,128)(2,1)}, bf16[1024,2048]{1,0:T(8,128)(2,1)}, u32[]{:S(2)}, u32[]{:S(2)}) collective-permute-start(bf16[1024,2048]{1,0:T(8,128)(2,1)} %get-tuple-element.4), channel_id=1, source_target_pairs={{254,0},{0,2},{2,4},{4,6},{6,8},{8,10},{10,12},{12,14},{14,16},{16... | collective-permute-start | bytes 12582920 | tf_op jit(solution)/shard_map/ppermute | solution.py:21
  198.8 206.2 %collective-permute-start.5 = (bf16[1024,2048]{1,0:T(8,128)(2,1)}, bf16[1024,2048]{1,0:T(8,128)(2,1)}, u32[]{:S(2)}, u32[]{:S(2)}) collective-permute-start(bf16[1024,2048]{1,0:T(8,128)(2,1)} %get-tuple-element.4), channel_id=1, source_target_pairs={{2,0},{4,2},{6,4},{8,6},{10,8},{12,10},{14,12},{16,14},{18,16},{20... | collective-permute-start | bytes 12582920 | tf_op jit(solution)/shard_map/ppermute | solution.py:21
  198.8 206.2 %collective-permute-start.2 = (bf16[1024,2048]{1,0:T(8,128)(2,1)}, bf16[1024,2048]{1,0:T(8,128)(2,1)}, u32[]{:S(2)}, u32[]{:S(2)}) collective-permute-start(bf16[1024,2048]{1,0:T(8,128)(2,1)} %get-tuple-element.3), channel_id=1, source_target_pairs={{254,0},{0,2},{2,4},{4,6},{6,8},{8,10},{10,12},{12,14},{14,16},{16... | collective-permute-start | bytes 12582920 | tf_op jit(solution)/shard_map/ppermute | solution.py:21
  208.2 188.0 %all-to-all-start.1 = ((f32[2,384,1024]{2,1,0:T(8,128)}), f32[2,384,1024]{2,1,0:T(8,128)}, u32[]{:S(2)}, u32[]{:S(2)}) async-start(f32[2,384,1024]{2,1,0:T(8,128)} %broadcast_in_dim.10), calls=%async_computation.1 | async-start | bytes 6291456 | tf_op jit(solution)/shard_map/all_to_all | solution.py:26
  221.7 183.4 %copy-start.1 = (bf16[1,384,1024]{2,1,0:T(8,128)(2,1)S(1)}, bf16[1,384,1024]{2,1,0:T(8,128)(2,1)}, u32[]{:S(2)}) copy-start(bf16[1,384,1024]{2,1,0:T(8,128)(2,1)} %all-gather) | copy-start | bytes 2359300
where the time goes:
time: 421 us; the launch traced here: 420 us
  blocking collectives  257 us (61%)
  starting transfers between devices  108 us (26%)
  matrix products  37.1 us (9%)
  other arithmetic  12.1 us (3%)
    psum x5, blocking collectives, over_axes(): return functools.reduce(lax.psum, axes, x)  179 us
    ppermute x6, starting transfers between devices, from_behind(): return lax.ppermute(block, axis, route)  94.4 us
    all_gather x1, blocking collectives, on_device(): full_targ = lax.all_gather(targ_local, 'mp', axis=1, tiled=True)  78.1 us
    dot_general x2, matrix products, gradient(): lax.dot_general(resid, feats, (((0,), (0,)), ((), ())), preferred_element...  29 us
    all_to_all x2, starting transfers between devices, from_everyone(): return lax.all_to_all(copies, axis, split_axis=0, concat_axis=0, tiled=True)  13.3 us
  transfers between devices with their start and end apart: 8, of which 0 were waited for; matrix products, arithmetic and copies ran while one was open for 6% of the time, Pallas kernels for 0%

commit v1 on v0

v1 whole, which is shorter than its diff:
```python
import functools

import jax
import jax.numpy as jnp
from jax import lax
from jax.experimental import pallas as pl
from jax.experimental.pallas import tpu as pltpu
from jax.sharding import Mesh
from jax.sharding import PartitionSpec as P

BLK = ("blk_0", "blk_1", "blk_2", "blk_3")
AXES = ("blk_0", "blk_1", "blk_2", "blk_3", "mp")
MESH = pl.DeviceIdType.MESH
f32 = jnp.float32
bf16 = jnp.bfloat16
mix_third = 1.0 / 3.0
step_size = 0.1

CHUNKS = (64, 32, 32)
TILE = 1024


def folded(value):
    rows, cols = value.shape
    total = None
    for i in range(0, rows, 8):
        for j in range(0, cols, 128):
            part = value[i : i + 8, j : j + 128]
            total = part if total is None else total + part
    return total


def kernel(dims, p_ref, h_ref, t_ref, out_ref, err_ref, *scratch):
    ny, nz, rows, width, tok, chunks = dims
    n = len(chunks)
    names = iter(scratch)
    H, TG, TT, EA, ES, ER, EZ, EY = (next(names) for _ in range(8))
    X0, X1, XH, G0, X2, ZS, ZR, RA, RB = ([next(names) for _ in range(n)] for _ in range(9))
    h_s, h_r, t_s, t_r, x_s, x_r, z_s, z_r, o_s, o_r, e_s, e_r, loc = names

    y, z = lax.axis_index("blk_0"), lax.axis_index("blk_1")
    xh, c, xl = lax.axis_index("blk_2"), lax.axis_index("blk_3"), lax.axis_index("mp")
    x = 2 * xh + xl
    b = 2 * x + c
    mine = 2 * xh + c
    k = y * nz + z
    starts = [sum(chunks[:j]) for j in range(n)]

    def ring(dx, dc):
        xd = lax.rem(x + dx, 4)
        return {"blk_2": lax.div(xd, 2), "mp": lax.rem(xd, 2), "blk_3": lax.rem(c + dc, 2)}

    def group(dk):
        kd = lax.rem(k + dk + ny * nz, ny * nz)
        return {"blk_0": lax.div(kd, nz), "blk_1": lax.rem(kd, nz)}

    def remote(src, dst, send, recv, to):
        return pltpu.make_async_remote_copy(
            src_ref=src, dst_ref=dst, send_sem=send, recv_sem=recv, device_id=to, device_id_type=MESH
        )

    offsets = [(2, 0), (2, 1), (1, 0), (3, 0), (1, 1), (3, 1), (0, 1)]
    partners = [ring(*o) for o in offsets] + [group(1), group(-1)]
    partners += [{"blk_1": lax.rem(z + d, nz)} for d in range(1, nz)]
    partners += [{"blk_0": lax.rem(y + d, ny)} for d in range(1, ny)]
    barrier = pltpu.get_barrier_semaphore()
    for to in partners:
        pl.semaphore_signal(barrier, inc=1, device_id=to, device_id_type=MESH)

    def slot(dx):
        xs = lax.rem(x + dx, 4)
        return (2 * lax.div(xs, 2) + c) * 2 + lax.rem(xs, 2)

    half = tok // 2
    first, second, whole = pl.ds(0, half), pl.ds(half, half), pl.ds(0, tok)

    def hidden_copy(i, dx, part, to, own=False):
        dst = H.at[slot(dx), part]
        return remote(h_ref.at[part] if own else dst, dst, h_s.at[i], h_r.at[i], to)

    ahead, behind, sibling = ring(1, 0), ring(3, 0), ring(0, 1)
    own_h = [
        hidden_copy(0, 0, first, ahead, True),
        hidden_copy(1, 0, second, behind, True),
        hidden_copy(2, 0, second, ahead, True),
        hidden_copy(3, 0, first, behind, True),
        hidden_copy(4, 0, whole, sibling, True),
    ]
    relay_h = [hidden_copy(5, 3, first, ahead), hidden_copy(6, 1, second, behind)]
    pass_h = [
        hidden_copy(7, 3, whole, sibling),
        hidden_copy(8, 1, whole, sibling),
        hidden_copy(9, 2, first, sibling),
        hidden_copy(10, 2, second, sibling),
    ]
    keep_h = pltpu.make_async_copy(h_ref, H.at[slot(0)], loc.at[0])

    lane = rows
    t_copies = []
    for m in range(4):
        xd, cd = 2 * xl + m // 2, m % 2
        src = t_ref.at[:, pl.ds(m * lane, lane)]
        own = jnp.logical_and(x == xd, c == cd)
        to = {"blk_2": lax.div(xd, 2), "mp": lax.rem(xd, 2), "blk_3": cd}
        t_copies.append(
            (
                own,
                remote(src, TG.at[mine], t_s.at[m], t_r.at[mine], to),
                pltpu.make_async_copy(src, TG.at[mine], loc.at[1]),
            )
        )

    def x_copies(j):
        out = []
        for i, (dx, dc) in enumerate(offsets):
            bd = 2 * lax.rem(x + dx, 4) + lax.rem(c + dc, 2)
            src = p_ref.at[pl.ds(pl.multiple_of(bd * rows + starts[j], 16), chunks[j])]
            out.append(remote(src, X0[j].at[1 + mine, xl], x_s.at[j, i], x_r.at[j, i], ring(dx, dc)))
        src = p_ref.at[pl.ds(pl.multiple_of(b * rows + starts[j], 16), chunks[j])]
        return out, pltpu.make_async_copy(src, X0[j].at[1 + mine, xl], loc.at[2 + j])

    x0 = [x_copies(j) for j in range(n)]

    def halo(j, q, direction, src, dst):
        return remote(src, dst, z_s.at[j, q, direction], z_r.at[j, q, direction], group(1 - 2 * direction))

    x0_halo = [
        (halo(j, 0, 0, X0[j].at[4], X0[j].at[0]), halo(j, 0, 1, X0[j].at[1], X0[j].at[5])) for j in range(n)
    ]
    z_halo = [
        (halo(j, 1, 0, ZS[j].at[0], ZR[j].at[1]), halo(j, 1, 1, ZS[j].at[1], ZR[j].at[0])) for j in range(n)
    ]
    x1_halo = [
        (halo(j, 2, 0, X1[j].at[3, 1], XH[j].at[1]), halo(j, 2, 1, X1[j].at[0, 0], XH[j].at[0])) for j in range(n)
    ]

    def back_copies(j):
        out = []
        for s in range(8):
            r, hf = s // 2, s % 2
            own = jnp.logical_and(x == 2 * (r // 2) + hf, c == r % 2)
            to = {"blk_2": r // 2, "mp": hf, "blk_3": r % 2}
            dst = out_ref.at[pl.ds(pl.multiple_of(b * rows + starts[j], 16), chunks[j])]
            out.append(
                (
                    own,
                    remote(X2[j].at[r, hf], dst, o_s.at[j, s], o_r.at[j, b], to),
                    pltpu.make_async_copy(X2[j].at[r, hf], dst, loc.at[2 + n + j]),
                )
            )
        return out

    back = [back_copies(j) for j in range(n)]

    def start_one(entry):
        own, away, near = entry
        pl.when(jnp.logical_not(own))(away.start)
        pl.when(own)(near.start)

    def finish_one(entry):
        own, away, near = entry
        pl.when(jnp.logical_not(own))(away.wait_send)
        pl.when(own)(near.wait)

    def forward(w_ref, base, t_start, size, out):
        def replica(r, carry):
            def part(hf, acc):
                return acc + lax.dot_general(
                    w_ref[r + base, hf], H[2 * r + hf], (((1,), (1,)), ((), ())), preferred_element_type=f32
                )

            acc = lax.fori_loop(0, 2, part, jnp.zeros((size, tok), f32))
            out[r] = (acc - TT[r, pl.ds(t_start, size)]).astype(bf16)
            return carry

        lax.fori_loop(0, 4, replica, 0)

    tiles = width // TILE

    def over_tiles(body):
        def step(i, carry):
            ii = lax.div(i, 2 * tiles)
            hf = lax.rem(lax.div(i, tiles), 2)
            cols = pl.ds(pl.multiple_of(lax.rem(i, tiles) * TILE, TILE), TILE)
            body(ii, hf, cols)
            return carry

        lax.fori_loop(0, 4 * tiles, step, 0)

    def grad(res, r, hf, cols):
        return lax.dot_general(
            res[r], H[2 * r + hf, :, cols], (((1,), (0,)), ((), ())), preferred_element_type=f32
        ) * (1.0 / tok)

    def update(j, r, hf, cols, where=None):
        g = grad(RA[j], r, hf, cols)
        G0[j][r, hf, :, cols] = g
        own = X0[j][r + 1, hf, :, cols].astype(f32)
        right = X0[j][r + 2, hf, :, cols].astype(f32)
        left = X0[j][r, hf, :, cols].astype(f32)
        diff = own - right
        EA[0] += folded(diff * diff)
        pull = step_size * g.astype(bf16).astype(f32)
        new = ((left + own + right) * mix_third - pull).astype(bf16)
        X1[j][r, hf, :, cols] = new
        if where is not None:
            ZS[j][where, hf, :, cols] = (new.astype(f32) - pull).astype(bf16)

    def stage_B(j):
        for copy in x0_halo[j]:
            copy.wait_recv()
        over_tiles(lambda i, hf, cols: update(j, 3 - 3 * i, hf, cols, i))
        for copy in z_halo[j] + x1_halo[j]:
            copy.start()
        over_tiles(lambda i, hf, cols: update(j, 1 + i, hf, cols))

    def inner(j, i, hf, cols):
        r = 1 + i
        own = X1[j][r, hf, :, cols].astype(f32)
        right = X1[j][r + 1, hf, :, cols].astype(f32)
        left = X1[j][r - 1, hf, :, cols].astype(f32)
        diff = own - right
        EA[1] += folded(diff * diff)
        g0 = G0[j][r, hf, :, cols]
        tracks = (
            G0[j][r - 1, hf, :, cols].astype(bf16).astype(f32)
            + g0.astype(bf16).astype(f32)
            + G0[j][r + 1, hf, :, cols].astype(bf16).astype(f32)
        )
        track = (tracks * mix_third + grad(RB[j], r, hf, cols) - g0).astype(bf16).astype(f32)
        X2[j][r, hf, :, cols] = ((left + own + right) * mix_third - step_size * track).astype(bf16)

    def outer(j, i, hf, cols):
        r, nb = 3 - 3 * i, 2 - i
        own = X1[j][r, hf, :, cols].astype(f32)
        near = X1[j][nb, hf, :, cols].astype(f32)
        far = XH[j][hf, :, cols].astype(f32)
        near_diff, far_diff = own - near, own - far
        near_weight = jnp.where(i == 1, 1.0, 0.0).astype(f32)
        far_weight = jnp.where(i == hf, 1.0, 0.0).astype(f32)
        EA[1] += folded(near_diff * near_diff) * near_weight + folded(far_diff * far_diff) * far_weight
        g0 = G0[j][r, hf, :, cols]
        tracks = g0.astype(bf16).astype(f32) + G0[j][nb, hf, :, cols].astype(bf16).astype(f32)
        mixed = (ZR[j][i, hf, :, cols].astype(f32) + own + near - step_size * tracks) * mix_third
        X2[j][r, hf, :, cols] = (mixed - step_size * (grad(RB[j], r, hf, cols) - g0)).astype(bf16)

    def stage_H(j):
        for copy in x0[j][0]:
            copy.wait_recv()
        x0[j][1].wait()
        for copy in x0_halo[j]:
            copy.start()

    def stage_A(j):
        forward(X0[j], 1, starts[j], chunks[j], RA[j])

    def stage_C(j):
        forward(X1[j], 0, starts[j], chunks[j], RB[j])

    def stage_I(j):
        over_tiles(functools.partial(inner, j))
        for s in (2, 3, 4, 5):
            start_one(back[j][s])

    def stage_O(j):
        for copy in z_halo[j] + x1_halo[j]:
            copy.wait_recv()
        over_tiles(functools.partial(outer, j))

    def send_outer(j):
        for s in (6, 7, 0, 1):
            start_one(back[j][s])

    def issue_x0(j):
        for copy in x0[j][0]:
            copy.start()
        x0[j][1].start()

    EA[...] = jnp.zeros_like(EA)
    pl.semaphore_wait(barrier, len(partners))

    issue_x0(0)
    for copy in own_h:
        copy.start()
    keep_h.start()
    for entry in t_copies:
        start_one(entry)
    stage_H(0)
    own_h[0].wait_recv()
    relay_h[0].start()
    own_h[1].wait_recv()
    relay_h[1].start()
    for j in range(1, n):
        issue_x0(j)
    for r in range(4):
        own = jnp.logical_and(r == mine, xl == xh)
        arrival = remote(TG.at[r], TG.at[r], t_s.at[0], t_r.at[r], sibling)
        pl.when(jnp.logical_not(own))(arrival.wait_recv)
    for entry in t_copies:
        finish_one(entry)

    def turn(r, carry):
        TT[r] = TG[r].astype(f32).T
        return carry

    lax.fori_loop(0, 4, turn, 0)
    own_h[2].wait_recv()
    pass_h[0].start()
    own_h[3].wait_recv()
    pass_h[1].start()
    relay_h[0].wait_recv()
    pass_h[2].start()
    relay_h[1].wait_recv()
    pass_h[3].start()
    own_h[4].wait_recv()
    for copy in pass_h:
        copy.wait_recv()
    keep_h.wait()

    stage_A(0)
    stage_B(0)
    stage_C(0)
    stage_I(0)
    for j in range(1, n):
        stage_H(j)
        stage_A(j)
        stage_B(j)
        stage_O(j - 1)
        send_outer(j - 1)
        stage_C(j)
        stage_I(j)
    stage_O(n - 1)

    sums = [jnp.sum(EA[i], axis=0, keepdims=True) for i in range(2)]
    row = lax.broadcasted_iota(jnp.int32, (8, 128), 0)
    ES[0] = jnp.where(row == 0, sums[0], jnp.where(row == 1, sums[1], 0.0))
    ER[b] = ES[0]
    e0 = []
    for i, (dx, dc) in enumerate(offsets):
        copy = remote(ES.at[0], ER.at[b], e_s.at[0, i], e_r.at[0, i], ring(dx, dc))
        copy.start()
        e0.append(copy)
    send_outer(n - 1)
    for copy in e0:
        copy.wait_recv()
    total = ER[0]
    for i in range(1, 8):
        total = total + ER[i]
    ES[1] = total
    EZ[z] = total
    e1 = []
    for d in range(1, nz):
        copy = remote(ES.at[1], EZ.at[z], e_s.at[1, d], e_r.at[1, d], {"blk_1": lax.rem(z + d, nz)})
        copy.start()
        e1.append(copy)
    for copy in e1:
        copy.wait_recv()
    total = EZ[0]
    for i in range(1, nz):
        total = total + EZ[i]
    ES[2] = total
    EY[y] = total
    e2 = []
    for d in range(1, ny):
        copy = remote(ES.at[2], EY.at[y], e_s.at[2, d], e_r.at[2, d], {"blk_0": lax.rem(y + d, ny)})
        copy.start()
        e2.append(copy)
    for copy in e2:
        copy.wait_recv()
    total = EY[0]
    for i in range(1, ny):
        total = total + EY[i]
    err_ref[...] = total

    for j in range(n):
        for s in range(8):
            arrival = remote(X2[j].at[0, 0], out_ref.at[pl.ds(starts[j], chunks[j])], o_s.at[j, 0], o_r.at[j, s], sibling)
            pl.when(s != b)(arrival.wait_recv)
    for copy in own_h + relay_h + pass_h + e0 + e1 + e2:
        copy.wait_send()
    for j in range(n):
        for copy in list(x0[j][0]) + list(x0_halo[j] + z_halo[j] + x1_halo[j]):
            copy.wait_send()
        for entry in back[j]:
            finish_one(entry)


def on_device(sizes, params, hidden, targets):
    ny, nz = sizes
    state, feats, targ = params[0], hidden[0], targets[0]
    depth, width = state.shape
    tok = feats.shape[0]
    rows = depth // 8
    n = len(CHUNKS)
    V, D = pltpu.VMEM, pltpu.SemaphoreType.DMA
    scratch = [
        V((8, tok, width), bf16),
        V((4, tok, rows), bf16),
        V((4, rows, tok), f32),
        V((2, 8, 128), f32),
        V((3, 8, 128), f32),
        V((8, 8, 128), f32),
        V((nz, 8, 128), f32),
        V((ny, 8, 128), f32),
    ]
    scratch += [V((6, 2, r, width), bf16) for r in CHUNKS]
    scratch += [V((4, 2, r, width), bf16) for r in CHUNKS]
    scratch += [V((2, r, width), bf16) for r in CHUNKS]
    scratch += [V((4, 2, r, width), f32) for r in CHUNKS]
    scratch += [V((4, 2, r, width), bf16) for r in CHUNKS]
    scratch += [V((2, 2, r, width), bf16) for r in CHUNKS]
    scratch += [V((2, 2, r, width), bf16) for r in CHUNKS]
    scratch += [V((4, r, tok), bf16) for r in CHUNKS]
    scratch += [V((4, r, tok), bf16) for r in CHUNKS]
    scratch += [D((11,)), D((11,)), D((4,)), D((4,)), D((n, 7)), D((n, 7)), D((n, 3, 2)), D((n, 3, 2))]
    scratch += [D((n, 8)), D((n, 8)), D((3, 8)), D((3, 8)), D((2 + 2 * n,))]
    anywhere = pl.BlockSpec(memory_space=pl.ANY)
    new_state, err = pl.pallas_call(
        functools.partial(kernel, (ny, nz, rows, width, tok, CHUNKS)),
        out_shape=(jax.ShapeDtypeStruct(state.shape, bf16), jax.ShapeDtypeStruct((8, 128), f32)),
        in_specs=[anywhere] * 3,
        out_specs=(anywhere, pl.BlockSpec(memory_space=pltpu.VMEM)),
        scratch_shapes=scratch,
        compiler_params=pltpu.CompilerParams(
            collective_id=0, has_side_effects=True, vmem_limit_bytes=60 * 2**20
        ),
    )(state, feats, targ)
    errors = jnp.sum(err[:2], axis=1) / (2 * width * 4 * ny * nz)
    return (new_state[None], errors)


def solution(mesh):
    torus = Mesh(mesh.devices.reshape(4, 8, 2, 2, mesh.shape["mp"]), AXES)
    placed = (P(BLK, None, "mp"), P(BLK, None, "mp"), P(BLK, None, "mp"))
    return jax.shard_map(
        functools.partial(on_device, (4, 8)),
        mesh=torus,
        in_specs=placed,
        out_specs=(P(BLK, None, "mp"), P()),
        check_vma=False,
    )
```

time: 421 us -> 188 us (0.45)
  the two profiles are of different devices: /device:TPU:194 before, /device:TPU:6 now
where the time goes in v1:
time: 188 us
  Pallas kernels  181 us (96%)
  local copies, waits for them, and re-layouts  4.79 us (3%)
    pallas_call x1, Pallas kernels, on_device(): pl.pallas_call(functools.partial(kernel, (ny, nz, rows, width, tok, CHUNK...  181 us
    unnamed x1, local copies, waits for them, and re-layouts  4.79 us

profile of v1, /device:TPU:6, one launch (start us, length us, event | category | flops | bytes accessed | tf_op | source)
XLA Modules:
  0.0 187.8 jit_solution(7660811884541304861)
XLA Ops:
  0.6 181.1 %shard_map.50 = (bf16[1024,2048]{1,0:T(8,128)(2,1)}, f32[8,128]{1,0:T(8,128)}) custom-call(bf16[1024,2048]{1,0:T(8,128)(2,1)} %bitcast.4, bf16[384,2048]{1,0:T(8,128)(2,1)} %bitcast.6, bf16[384,512]{1,0:T(8,128)(2,1)} %bitcast.7), custom_call_target="tpu_custom_call" | custom-call | tf_op jit(solution)/shard_map/pallas_call | solution.py:418
  181.7 0.8 slice_reduce_fusion
  182.5 0.5 broadcast_multiply_fusion
  183.0 4.8 %copy.6 = bf16[1,1024,2048]{2,1,0:T(8,128)(2,1)} copy(bf16[1,1024,2048]{2,1,0:T(8,128)(2,1)} %bitcast.5) | data formatting | bytes 8388608

commit v2 on v1

--- a/solution.py
+++ b/solution.py
@@ -16,8 +16,9 @@
 mix_third = 1.0 / 3.0
 step_size = 0.1
 
-CHUNKS = (64, 32, 32)
-TILE = 1024
+CHUNKS = (32, 48, 48)
+TILE = 2048
+ORDER = ("C0", "I0", "H1", "O0", "A1", "B1", "H2", "C1", "I1", "O1", "A2", "B2", "C2", "I2")
 
 
 def folded(value):
@@ -162,8 +163,10 @@
         pl.when(jnp.logical_not(own))(away.wait_send)
         pl.when(own)(near.wait)
 
-    def forward(w_ref, base, t_start, size, out):
-        def replica(r, carry):
+    def forward(w_ref, base, t_start, size, out, first=0, count=4):
+        def replica(i, carry):
+            r = first + i
+
             def part(hf, acc):
                 return acc + lax.dot_general(
                     w_ref[r + base, hf], H[2 * r + hf], (((1,), (1,)), ((), ())), preferred_element_type=f32
@@ -173,11 +176,11 @@
             out[r] = (acc - TT[r, pl.ds(t_start, size)]).astype(bf16)
             return carry
 
-        lax.fori_loop(0, 4, replica, 0)
+        lax.fori_loop(0, count, replica, 0)
 
     tiles = width // TILE
 
-    def over_tiles(body):
+    def over_tiles(body, count=2):
         def step(i, carry):
             ii = lax.div(i, 2 * tiles)
             hf = lax.rem(lax.div(i, tiles), 2)
@@ -185,7 +188,7 @@
             body(ii, hf, cols)
             return carry
 
-        lax.fori_loop(0, 4 * tiles, step, 0)
+        lax.fori_loop(0, 2 * count * tiles, step, 0)
 
     def grad(res, r, hf, cols):
         return lax.dot_general(
@@ -213,6 +216,19 @@
         for copy in z_halo[j] + x1_halo[j]:
             copy.start()
         over_tiles(lambda i, hf, cols: update(j, 1 + i, hf, cols))
+
+    def pair(side):
+        forward(X0[0], 1, 0, chunks[0], RA[0], 2 * side, 2)
+        edge = 1 - side
+        over_tiles(lambda i, hf, cols: update(0, 3 * side, hf, cols, edge), 1)
+        for way in range(2):
+
+            @pl.when(edge == way)
+            def _():
+                z_halo[0][way].start()
+                x1_halo[0][way].start()
+
+        over_tiles(lambda i, hf, cols: update(0, 1 + side, hf, cols), 1)
 
     def inner(j, i, hf, cols):
         r = 1 + i
@@ -308,27 +324,26 @@
     pass_h[0].start()
     own_h[3].wait_recv()
     pass_h[1].start()
+    own_h[4].wait_recv()
+    keep_h.wait()
+    pass_h[0].wait_recv()
+    pass_h[1].wait_recv()
+    for copy in x0_halo[0]:
+        copy.wait_recv()
+    pair(xh)
     relay_h[0].wait_recv()
     pass_h[2].start()
     relay_h[1].wait_recv()
     pass_h[3].start()
-    own_h[4].wait_recv()
-    for copy in pass_h:
-        copy.wait_recv()
-    keep_h.wait()
-
-    stage_A(0)
-    stage_B(0)
-    stage_C(0)
-    stage_I(0)
-    for j in range(1, n):
-        stage_H(j)
-        stage_A(j)
-        stage_B(j)
-        stage_O(j - 1)
-        send_outer(j - 1)
-        stage_C(j)
-        stage_I(j)
+    pass_h[2].wait_recv()
+    pass_h[3].wait_recv()
+    pair(1 - xh)
+
+    stages = {"H": stage_H, "A": stage_A, "B": stage_B, "C": stage_C, "I": stage_I, "O": stage_O}
+    for step in ORDER:
+        stages[step[0]](int(step[1]))
+        if step[0] == "O":
+            send_outer(int(step[1]))
     stage_O(n - 1)
 
     sums = [jnp.sum(EA[i], axis=0, keepdims=True) for i in range(2)]
@@ -370,7 +385,8 @@
     total = EY[0]
     for i in range(1, ny):
         total = total + EY[i]
-    err_ref[...] = total
+    for i in range(2):
+        err_ref[i] = jnp.sum(total[i : i + 1]) / (2 * width * 4 * ny * nz)
 
     for j in range(n):
         for s in range(8):
@@ -383,6 +399,26 @@
             copy.wait_send()
         for entry in back[j]:
             finish_one(entry)
+
+
+def settle(src, dst, hold, s_in, s_out):
+    parts = 8
+    size = src.shape[0] // parts
+    loads = [
+        pltpu.make_async_copy(src.at[pl.ds(i * size, size)], hold.at[pl.ds(i * size, size)], s_in.at[i])
+        for i in range(parts)
+    ]
+    stores = [
+        pltpu.make_async_copy(hold.at[pl.ds(i * size, size)], dst.at[pl.ds(i * size, size)], s_out.at[i])
+        for i in range(parts)
+    ]
+    for load in loads:
+        load.start()
+    for load, store in zip(loads, stores):
+        load.wait()
+        store.start()
+    for store in stores:
+        store.wait()
 
 
 def on_device(sizes, params, hidden, targets):
@@ -415,17 +451,23 @@
     scratch += [D((11,)), D((11,)), D((4,)), D((4,)), D((n, 7)), D((n, 7)), D((n, 3, 2)), D((n, 3, 2))]
     scratch += [D((n, 8)), D((n, 8)), D((3, 8)), D((3, 8)), D((2 + 2 * n,))]
     anywhere = pl.BlockSpec(memory_space=pl.ANY)
-    new_state, err = pl.pallas_call(
+    new_state, errors = pl.pallas_call(
         functools.partial(kernel, (ny, nz, rows, width, tok, CHUNKS)),
-        out_shape=(jax.ShapeDtypeStruct(state.shape, bf16), jax.ShapeDtypeStruct((8, 128), f32)),
+        out_shape=(jax.ShapeDtypeStruct(state.shape, bf16), jax.ShapeDtypeStruct((2,), f32)),
         in_specs=[anywhere] * 3,
-        out_specs=(anywhere, pl.BlockSpec(memory_space=pltpu.VMEM)),
+        out_specs=(anywhere, pl.BlockSpec(memory_space=pltpu.SMEM)),
         scratch_shapes=scratch,
         compiler_params=pltpu.CompilerParams(
             collective_id=0, has_side_effects=True, vmem_limit_bytes=60 * 2**20
         ),
     )(state, feats, targ)
-    errors = jnp.sum(err[:2], axis=1) / (2 * width * 4 * ny * nz)
+    new_state = pl.pallas_call(
+        settle,
+        out_shape=jax.ShapeDtypeStruct(state.shape, bf16),
+        in_specs=[anywhere],
+        out_specs=anywhere,
+        scratch_shapes=[V(state.shape, bf16), D((8,)), D((8,))],
+    )(new_state)
     return (new_state[None], errors)
 
 

time: 188 us -> 173 us (0.920)
  Pallas kernels: 181 us -> 172 us
  local copies, waits for them, and re-layouts: 4.79 us -> 0.52 us
    pallas_call x1, Pallas kernels: 181 us -> 168 us  [on_device(): pl.pallas_call(functools.partial(kernel, (ny, nz, rows, width, tok, CHUNK...]
    unnamed x1 -> x3, local copies, waits for them, and re-layouts: 4.79 us -> 0.52 us
    pallas_call x0 -> x1, Pallas kernels: none -> 3.58 us  [on_device(): pl.pallas_call(settle, out_shape=jax.ShapeDtypeStruct(state.shape, bf16),...]
where the time goes in v2:
time: 173 us
  Pallas kernels  172 us (99%)
    pallas_call x1, Pallas kernels, on_device(): pl.pallas_call(functools.partial(kernel, (ny, nz, rows, width, tok, CHUNK...  168 us
    pallas_call x1, Pallas kernels, on_device(): pl.pallas_call(settle, out_shape=jax.ShapeDtypeStruct(state.shape, bf16),...  3.58 us

profile of v2, /device:TPU:6, one launch (start us, length us, event | category | flops | bytes accessed | tf_op | source)
XLA Modules:
  0.0 172.9 jit_solution(15864753349445042111)
XLA Ops:
  0.6 168.1 %shard_map.50 = (bf16[1024,2048]{1,0:T(8,128)(2,1)}, f32[2]{0:T(128)}) custom-call(bf16[1024,2048]{1,0:T(8,128)(2,1)} %bitcast.4, bf16[384,2048]{1,0:T(8,128)(2,1)} %bitcast.6, bf16[384,512]{1,0:T(8,128)(2,1)} %bitcast.7), custom_call_target="tpu_custom_call" | custom-call | tf_op jit(solution)/shard_map/pallas_call | solution.py:454
  168.7 0.0 copy-start
  168.8 3.6 %shard_map.51 = bf16[1024,2048]{1,0:T(8,128)(2,1)} custom-call(bf16[1024,2048]{1,0:T(8,128)(2,1)} %get-tuple-element.4.src), custom_call_target="tpu_custom_call" | custom-call | tf_op jit(solution)/shard_map/pallas_call | solution.py:464
  172.3 0.0 copy-done
  172.3 0.5 copy.6
Async XLA Ops:
  168.7 3.6 %copy-start = (f32[2]{0:T(128)S(1)}, f32[2]{0:T(128)}, u32[]{:S(2)}) copy-start(f32[2]{0:T(128)} %get-tuple-element.9) | copy-start | bytes 28

commit v3 on v2

--- a/solution.py
+++ b/solution.py
@@ -18,7 +18,8 @@
 
 CHUNKS = (32, 48, 48)
 TILE = 2048
-ORDER = ("C0", "I0", "H1", "O0", "A1", "B1", "H2", "C1", "I1", "O1", "A2", "B2", "C2", "I2")
+ORDER = ("F0", "J0", "H2", "P0", "F1", "J1", "U2", "C2", "I2", "O1")
+EARLY = 2
 
 
 def folded(value):
@@ -192,11 +193,11 @@
 
     def grad(res, r, hf, cols):
         return lax.dot_general(
-            res[r], H[2 * r + hf, :, cols], (((1,), (0,)), ((), ())), preferred_element_type=f32
+            res, H[2 * r + hf, :, cols], (((1,), (0,)), ((), ())), preferred_element_type=f32
         ) * (1.0 / tok)
 
-    def update(j, r, hf, cols, where=None):
-        g = grad(RA[j], r, hf, cols)
+    def update(j, r, hf, cols, where=None, g=None):
+        g = grad(RA[j][r], r, hf, cols) if g is None else g
         G0[j][r, hf, :, cols] = g
         own = X0[j][r + 1, hf, :, cols].astype(f32)
         right = X0[j][r + 2, hf, :, cols].astype(f32)
@@ -230,8 +231,9 @@
 
         over_tiles(lambda i, hf, cols: update(0, 1 + side, hf, cols), 1)
 
-    def inner(j, i, hf, cols):
+    def inner(j, i, hf, cols, g=None):
         r = 1 + i
+        g = grad(RB[j][r], r, hf, cols) if g is None else g
         own = X1[j][r, hf, :, cols].astype(f32)
         right = X1[j][r + 1, hf, :, cols].astype(f32)
         left = X1[j][r - 1, hf, :, cols].astype(f32)
@@ -243,11 +245,12 @@
             + g0.astype(bf16).astype(f32)
             + G0[j][r + 1, hf, :, cols].astype(bf16).astype(f32)
         )
-        track = (tracks * mix_third + grad(RB[j], r, hf, cols) - g0).astype(bf16).astype(f32)
+        track = (tracks * mix_third + g - g0).astype(bf16).astype(f32)
         X2[j][r, hf, :, cols] = ((left + own + right) * mix_third - step_size * track).astype(bf16)
 
-    def outer(j, i, hf, cols):
+    def outer(j, i, hf, cols, g=None):
         r, nb = 3 - 3 * i, 2 - i
+        g = grad(RB[j][r], r, hf, cols) if g is None else g
         own = X1[j][r, hf, :, cols].astype(f32)
         near = X1[j][nb, hf, :, cols].astype(f32)
         far = XH[j][hf, :, cols].astype(f32)
@@ -258,7 +261,7 @@
         g0 = G0[j][r, hf, :, cols]
         tracks = g0.astype(bf16).astype(f32) + G0[j][nb, hf, :, cols].astype(bf16).astype(f32)
         mixed = (ZR[j][i, hf, :, cols].astype(f32) + own + near - step_size * tracks) * mix_third
-        X2[j][r, hf, :, cols] = (mixed - step_size * (grad(RB[j], r, hf, cols) - g0)).astype(bf16)
+        X2[j][r, hf, :, cols] = (mixed - step_size * (g - g0)).astype(bf16)
 
     def stage_H(j):
         for copy in x0[j][0]:
@@ -282,6 +285,57 @@
         for copy in z_halo[j] + x1_halo[j]:
             copy.wait_recv()
         over_tiles(functools.partial(outer, j))
+
+    def both(j, r, hf, cols):
+        res = jnp.concatenate([RB[j][r], RA[j + 1][r]], axis=0)
+        g = grad(res, r, hf, cols)
+        return g[: chunks[j]], g[chunks[j] :]
+
+    def stage_F(j):
+        size = chunks[j]
+
+        def replica(r, carry):
+            def part(hf, acc):
+                w = jnp.concatenate([X1[j][r, hf], X0[j + 1][r + 1, hf]], axis=0)
+                return acc + lax.dot_general(w, H[2 * r + hf], (((1,), (1,)), ((), ())), preferred_element_type=f32)
+
+            acc = lax.fori_loop(0, 2, part, jnp.zeros((size + chunks[j + 1], tok), f32))
+            RB[j][r] = (acc[:size] - TT[r, pl.ds(starts[j], size)]).astype(bf16)
+            RA[j + 1][r] = (acc[size:] - TT[r, pl.ds(starts[j + 1], chunks[j + 1])]).astype(bf16)
+            return carry
+
+        lax.fori_loop(0, 4, replica, 0)
+
+    def stage_J(j):
+        def body(i, hf, cols):
+            g1, g0 = both(j, 1 + i, hf, cols)
+            inner(j, i, hf, cols, g1)
+            update(j + 1, 1 + i, hf, cols, None, g0)
+
+        over_tiles(body)
+        for s in (2, 3, 4, 5):
+            start_one(back[j][s])
+
+    def stage_P(j):
+        for copy in z_halo[j] + x1_halo[j] + x0_halo[j + 1]:
+            copy.wait_recv()
+
+        def body(i, hf, cols):
+            g1, g0 = both(j, 3 - 3 * i, hf, cols)
+            outer(j, i, hf, cols, g1)
+            update(j + 1, 3 - 3 * i, hf, cols, i, g0)
+
+        over_tiles(body)
+        for copy in z_halo[j + 1] + x1_halo[j + 1]:
+            copy.start()
+        send_outer(j)
+
+    def stage_U(j):
+        for copy in x0_halo[j]:
+            copy.wait_recv()
+        over_tiles(lambda i, hf, cols: update(j, 3 - 3 * i, hf, cols, i))
+        for copy in z_halo[j] + x1_halo[j]:
+            copy.start()
 
     def send_outer(j):
         for s in (6, 7, 0, 1):
@@ -303,10 +357,12 @@
         start_one(entry)
     stage_H(0)
     own_h[0].wait_recv()
+    for j in range(1, EARLY):
+        issue_x0(j)
     relay_h[0].start()
     own_h[1].wait_recv()
     relay_h[1].start()
-    for j in range(1, n):
+    for j in range(EARLY, n):
         issue_x0(j)
     for r in range(4):
         own = jnp.logical_and(r == mine, xl == xh)
@@ -331,6 +387,8 @@
     for copy in x0_halo[0]:
         copy.wait_recv()
     pair(xh)
+    for j in range(1, EARLY):
+        stage_H(j)
     relay_h[0].wait_recv()
     pass_h[2].start()
     relay_h[1].wait_recv()
@@ -339,7 +397,8 @@
     pass_h[3].wait_recv()
     pair(1 - xh)
 
-    stages = {"H": stage_H, "A": stage_A, "B": stage_B, "C": stage_C, "I": stage_I, "O": stage_O}
+    stages = {"F": stage_F, "J": stage_J, "P": stage_P, "U": stage_U}
+    stages |= {"H": stage_H, "A": stage_A, "B": stage_B, "C": stage_C, "I": stage_I, "O": stage_O}
     for step in ORDER:
         stages[step[0]](int(step[1]))
         if step[0] == "O":

time: 173 us -> 171 us (0.988)
  Pallas kernels: 172 us -> 170 us
    pallas_call x1, Pallas kernels: 168 us -> 166 us  [on_device(): pl.pallas_call(functools.partial(kernel, (ny, nz, rows, width, tok, CHUNK...]
where the time goes in v3:
time: 171 us
  Pallas kernels  170 us (99%)
    pallas_call x1, Pallas kernels, on_device(): pl.pallas_call(functools.partial(kernel, (ny, nz, rows, width, tok, CHUNK...  166 us
    pallas_call x1, Pallas kernels, on_device(): pl.pallas_call(settle, out_shape=jax.ShapeDtypeStruct(state.shape, bf16),...  3.58 us

profile of v3, /device:TPU:6, one launch (start us, length us, event | category | flops | bytes accessed | tf_op | source)
XLA Modules:
  0.0 170.9 jit_solution(17350371021482119476)
XLA Ops:
  0.6 166.1 %shard_map.50 = (bf16[1024,2048]{1,0:T(8,128)(2,1)}, f32[2]{0:T(128)}) custom-call(bf16[1024,2048]{1,0:T(8,128)(2,1)} %bitcast.4, bf16[384,2048]{1,0:T(8,128)(2,1)} %bitcast.6, bf16[384,512]{1,0:T(8,128)(2,1)} %bitcast.7), custom_call_target="tpu_custom_call" | custom-call | tf_op jit(solution)/shard_map/pallas_call | solution.py:513
  166.8 0.0 copy-start
  166.8 3.6 %shard_map.51 = bf16[1024,2048]{1,0:T(8,128)(2,1)} custom-call(bf16[1024,2048]{1,0:T(8,128)(2,1)} %get-tuple-element.4.src), custom_call_target="tpu_custom_call" | custom-call | tf_op jit(solution)/shard_map/pallas_call | solution.py:523
  170.4 0.0 copy-done
  170.4 0.5 copy.6
Async XLA Ops:
  166.8 3.6 %copy-start = (f32[2]{0:T(128)S(1)}, f32[2]{0:T(128)}, u32[]{:S(2)}) copy-start(f32[2]{0:T(128)} %get-tuple-element.9) | copy-start | bytes 28

commit v4 on v3

--- a/solution.py
+++ b/solution.py
@@ -254,10 +254,14 @@
         own = X1[j][r, hf, :, cols].astype(f32)
         near = X1[j][nb, hf, :, cols].astype(f32)
         far = XH[j][hf, :, cols].astype(f32)
-        near_diff, far_diff = own - near, own - far
-        near_weight = jnp.where(i == 1, 1.0, 0.0).astype(f32)
-        far_weight = jnp.where(i == hf, 1.0, 0.0).astype(f32)
-        EA[1] += folded(near_diff * near_diff) * near_weight + folded(far_diff * far_diff) * far_weight
+        if j == n - 1:
+            near_diff = far_diff = None
+        else:
+            near_diff, far_diff = own - near, own - far
+        if near_diff is not None:
+            near_weight = jnp.where(i == 1, 1.0, 0.0).astype(f32)
+            far_weight = jnp.where(i == hf, 1.0, 0.0).astype(f32)
+            EA[1] += folded(near_diff * near_diff) * near_weight + folded(far_diff * far_diff) * far_weight
         g0 = G0[j][r, hf, :, cols]
         tracks = g0.astype(bf16).astype(f32) + G0[j][nb, hf, :, cols].astype(bf16).astype(f32)
         mixed = (ZR[j][i, hf, :, cols].astype(f32) + own + near - step_size * tracks) * mix_third
@@ -403,8 +407,19 @@
         stages[step[0]](int(step[1]))
         if step[0] == "O":
             send_outer(int(step[1]))
-    stage_O(n - 1)
-
+    last = n - 1
+    for copy in z_halo[last] + x1_halo[last]:
+        copy.wait_recv()
+
+    def last_edges(i, carry):
+        hf = lax.div(i, tiles)
+        cols = pl.ds(pl.multiple_of(lax.rem(i, tiles) * TILE, TILE), TILE)
+        near = X1[last][0, hf, :, cols].astype(f32) - X1[last][1, hf, :, cols].astype(f32)
+        far = X1[last][3 - 3 * hf, hf, :, cols].astype(f32) - XH[last][hf, :, cols].astype(f32)
+        EA[1] += folded(near * near) + folded(far * far)
+        return carry
+
+    lax.fori_loop(0, 2 * tiles, last_edges, 0)
     sums = [jnp.sum(EA[i], axis=0, keepdims=True) for i in range(2)]
     row = lax.broadcasted_iota(jnp.int32, (8, 128), 0)
     ES[0] = jnp.where(row == 0, sums[0], jnp.where(row == 1, sums[1], 0.0))
@@ -414,7 +429,8 @@
         copy = remote(ES.at[0], ER.at[b], e_s.at[0, i], e_r.at[0, i], ring(dx, dc))
         copy.start()
         e0.append(copy)
-    send_outer(n - 1)
+    over_tiles(functools.partial(outer, last))
+    send_outer(last)
     for copy in e0:
         copy.wait_recv()
     total = ER[0]

time: 171 us -> 169 us (0.988); the launches traced: 171 us -> 167 us
  Pallas kernels: 170 us -> 166 us
    pallas_call x1, Pallas kernels: 166 us -> 162 us  [on_device(): pl.pallas_call(functools.partial(kernel, (ny, nz, rows, width, tok, CHUNK...]
where the time goes in v4:
time: 169 us; the launch traced here: 167 us
  Pallas kernels  166 us (98%)
    pallas_call x1, Pallas kernels, on_device(): pl.pallas_call(functools.partial(kernel, (ny, nz, rows, width, tok, CHUNK...  162 us
    pallas_call x1, Pallas kernels, on_device(): pl.pallas_call(settle, out_shape=jax.ShapeDtypeStruct(state.shape, bf16),...  3.58 us

profile of v4, /device:TPU:6, one launch (start us, length us, event | category | flops | bytes accessed | tf_op | source)
XLA Modules:
  0.0 166.8 jit_solution(1779425097793243411)
XLA Ops:
  0.6 162.0 %shard_map.50 = (bf16[1024,2048]{1,0:T(8,128)(2,1)}, f32[2]{0:T(128)}) custom-call(bf16[1024,2048]{1,0:T(8,128)(2,1)} %bitcast.4, bf16[384,2048]{1,0:T(8,128)(2,1)} %bitcast.6, bf16[384,512]{1,0:T(8,128)(2,1)} %bitcast.7), custom_call_target="tpu_custom_call" | custom-call | tf_op jit(solution)/shard_map/pallas_call | solution.py:529
  162.6 0.0 copy-start
  162.6 3.6 %shard_map.51 = bf16[1024,2048]{1,0:T(8,128)(2,1)} custom-call(bf16[1024,2048]{1,0:T(8,128)(2,1)} %get-tuple-element.4.src), custom_call_target="tpu_custom_call" | custom-call | tf_op jit(solution)/shard_map/pallas_call | solution.py:539
  166.2 0.0 copy-done
  166.2 0.5 copy.6
Async XLA Ops:
  162.6 3.6 %copy-start = (f32[2]{0:T(128)S(1)}, f32[2]{0:T(128)}, u32[]{:S(2)}) copy-start(f32[2]{0:T(128)} %get-tuple-element.9) | copy-start | bytes 28
